TPU v7x, 256 devices: a whole 4x4x8 slice. The times are simulated.
256 devices in a mesh: tm: 64 (over y, z, core), space: 4 (over x).
Axes of the slice: x: 4, y: 4, z: 8, core: 2. Of those that a mesh axis runs over, the one named last changes fastest.
Arguments:
- starts: float32 [64, 5, 16, 64, 128], P('tm', None, 'space'), may hold values from -4 to 4
- source: float32 [5, 16, 64, 128], P(None, 'space'), may hold values from -4 to 4
Outputs:
- ends: float32 [64, 5, 16, 64, 128], P('tm', None, 'space')
- slice_norms: float32 [64], P('tm')
- total_norm: float32 [1], replicated
All inputs are finite; a program needn't handle non-finite values.
Results may differ from a plain program's by a relative error of at most 0.0003.
Values sent between devices are 32-bit elements; how exact they have to be, the bound alone decides.
A program may use at most 64 MiB of HBM per device.

v0:
```python
import functools
import math

import jax
import jax.numpy as jnp
import numpy as np
from jax import lax
from jax.experimental import pallas as pl
from jax.experimental.pallas import tpu as pltpu
from jax.sharding import Mesh
from jax.sharding import PartitionSpec as P

Y, Z, C, X = "tm_0", "tm_1", "tm_2", "space"
TM = (Y, Z, C)
MESH = pl.DeviceIdType.MESH
F32, BF16 = jnp.float32, jnp.bfloat16

FIELDS, NZ, NY, NX, SLICES = 5, 16, 64, 128, 64
SLABS, DEPTH = 4, 4
KX, KY = NX // 16, NY // 8
CELLS = NZ * NY * NX
viscosity, diffusivity, compress_rate = 0.08, 0.05, 0.25
time_step, diffusion_number = 0.5, 0.08
advect = {"x": 0.2, "y": 0.15, "z": 0.1}
epsilon = 1e-06
GREETINGS = (None, 2, 6, 10, 14, 18, 22, 26)
PASS_ON = 18
QUARTERS = 4
ROWS = FIELDS * KX
Q_LANE, T_LANE = 64, 72


def halves(table):
    table = np.asarray(table, np.float32)
    high = table.astype(BF16)
    low = (table - high.astype(np.float32)).astype(BF16)
    return high, low


def tables():
    kx, xs = np.arange(KX), np.arange(NX)
    ky = (np.arange(2 * KY) + KY) % (2 * KY) - KY
    keep = (ky != -KY).astype(np.float64)
    ax = 2 * np.pi / NX * np.outer(kx, xs)
    cx = np.concatenate([np.cos(ax), np.sin(ax)])
    weight = np.where(kx == 0, 1.0, 2.0)[:, None]
    cinv = np.concatenate([weight * np.cos(ax), weight * np.sin(ax)])
    permuted = np.arange(NY).reshape(8, 8).T.reshape(-1)
    eye = np.eye(DEPTH)

    def plane(ys):
        ay = 2 * np.pi / NY * np.outer(ys, ky)
        return np.cos(ay) * keep, np.sin(ay) * keep

    co, si = plane(permuted)
    m1 = np.zeros((2, DEPTH, NY, DEPTH, 2, 2 * KY))
    for cs, (re, im) in enumerate(((co, -si), (-si, -co))):
        m1[cs, :, :, :, 0, :] = np.einsum("ab,yk->aybk", eye, re)
        m1[cs, :, :, :, 1, :] = np.einsum("ab,yk->aybk", eye, im)
    co, si = plane(np.arange(NY))
    m4 = np.zeros((DEPTH, 2, 2 * KY, 2, DEPTH, NY))
    for cs, (re, im) in enumerate(((co, -si), (-si, -co))):
        m4[:, 0, :, cs, :, :] = np.einsum("ab,yk->akby", eye, re) / CELLS
        m4[:, 1, :, cs, :, :] = np.einsum("ab,yk->akby", eye, im) / CELLS
    m1 = m1.reshape(512, DEPTH, 2, QUARTERS, 4).transpose(0, 3, 1, 2, 4)
    m4 = m4.reshape(DEPTH, 2, QUARTERS, 4, 512).transpose(2, 0, 1, 3, 4)
    zs, kz = np.arange(NZ), np.arange(NZ)
    az = 2 * np.pi / NZ * np.outer(zs, kz)
    same = np.eye(2 * KY) * keep
    m2 = np.zeros((NZ, 2, 2 * KY, 2, NZ, 2 * KY))
    m3 = np.zeros((2, NZ, 2 * KY, NZ, 2, 2 * KY))
    for i, o, fwd in ((0, 0, np.cos(az)), (0, 1, -np.sin(az)), (1, 0, np.sin(az)), (1, 1, np.cos(az))):
        m2[:, i, :, o, :, :] = np.einsum("zq,kl->zkql", fwd, same)
        m3[o, :, :, :, i, :] = np.einsum("zq,kl->qkzl", fwd, same)
    kzs = (kz + NZ // 2) % NZ - NZ // 2
    tz, ty = 2 * np.pi / NZ * kzs, 2 * np.pi / NY * ky
    tx = 2 * np.pi / NX * kx
    real = 1.0 + diffusion_number * (
        (2 * np.cos(tz) - 2)[None, :, None] + (2 * np.cos(ty) - 2)[None, None, :] + (2 * np.cos(tx) - 2)[:, None, None]
    )
    imag = -(
        advect["z"] * np.sin(tz)[None, :, None] + advect["y"] * np.sin(ty)[None, None, :] + advect["x"] * np.sin(tx)[:, None, None]
    )
    g = ((real + 1j * imag) * keep).reshape(KX, NZ * 2 * KY)
    powers = np.zeros((KX, 8, 2 * NZ * 2 * KY))
    for p in range(6):
        power = g ** (2**p)
        powers[:, p] = np.concatenate([power.real, power.imag], axis=1)
    m2 = m2.reshape(SLABS, DEPTH, 2, QUARTERS, 4, 512).transpose(0, 3, 1, 2, 4, 5)
    m3 = m3.reshape(512, SLABS, DEPTH, 2, QUARTERS, 4).transpose(0, 1, 4, 2, 3, 5)
    return dict(
        cx=np.concatenate(halves(cx)),
        m1=np.stack(halves(m1.reshape(512, 128))),
        m2=np.stack(halves(m2.reshape(512, 512))),
        m3=np.stack(halves(m3.reshape(512, 512))),
        powers=powers.astype(np.float32),
        m4=np.stack(halves(m4.reshape(128, 512))),
        cinv=np.concatenate([halves(cinv)[0], halves(cinv)[0], halves(cinv)[1]]),
    )


def split(x):
    high = x.astype(BF16)
    return high, (x - high.astype(F32)).astype(BF16)


def dot(a, b, dims=((1,), (0,))):
    return lax.dot_general(a, b, (dims, ((), ())), preferred_element_type=F32)


def product(x, high, low):
    m = x.shape[0]
    xh, xl = split(x)
    both = dot(jnp.concatenate([xh, xl], axis=0), high)
    return both[:m] + both[m:] + dot(xh, low)


def low_modes(field_rows, cx, m1):
    out = []
    for f in range(FIELDS):
        high, low = split(field_rows(f))
        a = dot(cx, high, ((1,), (1,)))
        a = a[:16] + a[16:] + dot(cx[:16], low, ((1,), (1,)))
        out.append(jnp.concatenate([a[:KX], a[KX:]], axis=1))
    return product(jnp.concatenate(out, axis=0), m1[0], m1[1])


def rem(a, n):
    return lax.rem(a, jnp.int32(n))


def picked(i, values):
    out = jnp.int32(values[-1])
    for k, v in enumerate(values[:-1]):
        out = jnp.where(i == k, jnp.int32(v), out)
    return out


def main_kernel(
    starts, source, cx_h, m1_h, m2_h, m3_h, pw_h,
    fine_out, back_out,
    st, sr, q, halo, fo, fn, cx, m1, m2, m3, pw,
    spec_s, after, spec_f, got, turn, back,
    in_sem, const_sem, out_sem, hs, hr, rounds, p_send, p_recv, f_send, f_recv, c_send, c_recv,
):
    x, y, z, c = (lax.axis_index(a) for a in (X, Y, Z, C))
    at = lambda x=x, y=y, z=z, c=c: {Y: y, Z: z, C: c, X: x}
    up, down = at(x=rem(x + 1, 4)), at(x=rem(x + 3, 4))
    load_s = [
        pltpu.make_async_copy(starts.at[0, :, pl.ds(p, n)], st.at[:, pl.ds(p, n)], in_sem.at[i])
        for i, (p, n) in ((0, (0, 1)), (0, (3, 1)), (1, (1, 2)))
    ]
    load_r = pltpu.make_async_copy(source, sr, in_sem.at[2])
    for copy in load_s[:2]:
        copy.start()
    consts = [
        pltpu.make_async_copy(a, b, const_sem.at[i])
        for i, (a, b) in ((0, (cx_h, cx)), (0, (m1_h, m1)), (1, (m2_h, m2)), (1, (m3_h, m3)))
    ]
    scan_x2z = x * 2 + rem(z, 2)
    load_p = pltpu.make_async_copy(pw_h.at[scan_x2z], pw, const_sem.at[1])

    barrier = pltpu.get_barrier_semaphore()
    around = [
        up, down, at(y=rem(y + 1, 4)), at(y=rem(y + 3, 4)), at(z=rem(z + 1, 8)), at(z=rem(z + 7, 8)), at(c=1 - c),
    ]
    for device in around:
        pl.semaphore_signal(barrier, inc=1, device_id=device, device_id_type=MESH)

    def greet(k):
        for turn_by in (1, -1):
            device = (
                at(x=rem(x + turn_by + 4, 4)), at(c=1 - c),
                at(y=rem(y + turn_by + 4, 4)), at(y=rem(y + turn_by + 4, 4)),
                *[at(z=rem(z + turn_by + 8, 8))] * 4,
            )[k]
            pl.semaphore_signal(rounds.at[k], inc=1, device_id=device, device_id_type=MESH)

    load_s[0].wait()
    load_s[1].wait()
    load_s[2].start()

    def lay(planes):
        def body(r, carry):
            for plane in planes:
                for f in range(FIELDS):
                    q[0, r + 1, plane, f] = st[f, plane, pl.ds(r, 8, stride=8), :]
            return carry
        lax.fori_loop(0, 8, body, 0)

    def edges(j, last):
        for plane in range(DEPTH):
            for f in range(FIELDS):
                if last:
                    q[j, 0, plane, f] = pltpu.roll(q[j, 8, plane, f], 1, 0)
                else:
                    q[j, 9, plane, f] = pltpu.roll(q[j, 1, plane, f], 7, 0)

    def sends(j, r):
        return (
            pltpu.make_async_remote_copy(
                q.at[j, r + 1, 0], halo.at[j, 1, r], hs, hr.at[j % 2, r], device_id=down, device_id_type=MESH
            ),
            pltpu.make_async_remote_copy(
                q.at[j, r + 1, DEPTH - 1], halo.at[j, 0, r], hs, hr.at[j % 2, r], device_id=up, device_id_type=MESH
            ),
        )

    lay((0, 3))
    pl.semaphore_wait(barrier, len(around))
    greet(0)

    def first(r, carry):
        for copy in sends(0, r):
            copy.start()
        return carry
    lax.fori_loop(0, 8, first, 0)
    for copy in (*consts[:2], load_r, *consts[2:], load_p):
        copy.start()
    load_s[2].wait()
    lay((1, 2))
    edges(0, False)
    edges(0, True)

    consts[0].wait()
    consts[1].wait()
    spec_s[...] = low_modes(
        lambda f: jnp.concatenate([q[0, 1:9, p, f].reshape(NY, NX) for p in range(DEPTH)], axis=0), cx[...], m1
    )
    load_r.wait()

    is_owner = c == 1
    has_two = is_owner & (y == rem(scan_x2z, 4))
    mine = (y * 8 + z) * 2 + c

    before = rem(mine + SLICES - 1, SLICES)
    pass_on = pltpu.make_async_remote_copy(
        spec_s, after, p_send, p_recv,
        device_id=at(y=lax.div(before, jnp.int32(16)), z=rem(lax.div(before, jnp.int32(2)), 8), c=rem(before, 2)),
        device_id_type=MESH,
    )

    def spread(tz):
        slot = x * SLICES + rem(mine + 1, SLICES)
        for dx in (2, 1, 3, 0):
            tx = rem(x + dx, 4)
            kx = tx * 2 + rem(tz, 2)
            for dy in (2, 1, 3, 0, None):
                ty = rem(kx, 4) if dy is None else rem(y + dy, 4)
                row = (32 if dy is None else ty * KX) + kx
                here = spec_f.at[pl.ds(row, 1)]
                there = got.at[pl.ds(slot + (SLABS * SLICES if dy is None else 0), 1)]

                def far():
                    pltpu.make_async_remote_copy(
                        here, there, f_send, f_recv, device_id=at(tx, ty, tz, jnp.int32(1)), device_id_type=MESH
                    ).start()

                if dx or dy:
                    far()
                    continue
                own = (tz == z) & (ty == y) & is_owner
                pl.when(jnp.logical_not(own))(far)

                @pl.when(own)
                def _():
                    pltpu.make_async_copy(here, there, f_recv).start()

    def stage(j):
        def body(i, carry):
            r = rem(i + j, 8)
            pltpu.make_async_copy(halo.at[j, :, r], halo.at[j, :, r], hr.at[j % 2, r]).wait()
            for k, turn_at in enumerate(GREETINGS):
                if turn_at is None or turn_at // 8 != j:
                    continue

                @pl.when(i == turn_at % 8)
                def _():
                    pl.semaphore_wait(rounds.at[k - 1], 2)
                    greet(k)
                    if turn_at == PASS_ON:
                        pass_on.start()

            for plane in (0, 3, 1, 2):
                cur = [q[j, r + 1, plane, f] for f in range(FIELDS)]
                yp = [q[j, r + 2, plane, f] for f in range(FIELDS)]
                ym = [q[j, r, plane, f] for f in range(FIELDS)]
                zp = [(halo[j, 1, r, f] if plane == 3 else q[j, r + 1, plane + 1, f]) for f in range(FIELDS)]
                zm = [(halo[j, 0, r, f] if plane == 0 else q[j, r + 1, plane - 1, f]) for f in range(FIELDS)]

                def flux(v, axis, sign):
                    half = 0.5 * advect["xyz"[axis]] + 0.5 * v[axis]
                    a = viscosity - half if sign > 0 else viscosity + half
                    b = diffusivity - half if sign > 0 else diffusivity + half
                    out = [a * v[0], a * v[1], a * v[2], b * v[4]]
                    push = 0.5 * v[3]
                    out[axis] = out[axis] - push if sign > 0 else out[axis] + push
                    return out

                xplus = [pltpu.roll(v, NX - 1, 1) for v in flux(cur, 0, 1)]
                xminus = [pltpu.roll(v, 1, 1) for v in flux(cur, 0, -1)]
                parts = (xplus, xminus, flux(yp, 1, 1), flux(ym, 1, -1), flux(zp, 2, 1), flux(zm, 2, -1))
                diverge = (
                    (pltpu.roll(cur[0], NX - 1, 1) - pltpu.roll(cur[0], 1, 1)) + (yp[1] - ym[1]) + (zp[2] - zm[2])
                )
                src = [sr[f, plane, pl.ds(r, 8, stride=8), :] for f in range(FIELDS)]
                rates = [None] * FIELDS
                for n, f in enumerate((0, 1, 2, 4)):
                    coefficient = -6.0 * (viscosity if f < 3 else diffusivity)
                    total = coefficient * cur[f] + src[f]
                    pairs = [p[n] for p in parts]
                    rates[f] = total + ((pairs[0] + pairs[1]) + (pairs[2] + pairs[3]) + (pairs[4] + pairs[5]))
                rates[3] = src[3] - (0.5 * compress_rate) * diverge
                for f in range(FIELDS):
                    begin = q[0, r + 1, plane, f]
                    if j < 3:
                        step = time_step * (0.5 if j < 2 else 1.0)
                        q[j + 1, r + 1, plane, f] = begin + step * rates[f]
                    else:
                        two = q[2, r + 1, plane, f]
                        states = (q[1, r + 1, plane, f] + two) + (two + cur[f]) - begin
                        fo[f, plane, pl.ds(pl.multiple_of(r * 8, 8), 8), :] = (1.0 / 3.0) * states + (
                            time_step / 6.0
                        ) * rates[f]
            if j < 3:
                for copy in sends(j + 1, r):
                    copy.start()
                pl.when(r == 0)(lambda: edges(j + 1, False))
                pl.when(r == 7)(lambda: edges(j + 1, True))
            return carry
        lax.fori_loop(0, 8, body, 0)

    for j in range(4):
        stage(j)
    pl.semaphore_wait(rounds.at[7], 2)

    modes = low_modes(lambda f: fo[f].reshape(DEPTH * NY, NX), cx[...], m1)
    pass_on.wait_recv()
    spec_f[...] = modes - after[...]

    def fine_rows(i, carry):
        spread(picked(i, (0, 1, 7, 2, 6, 3, 5, 4)))
        return carry
    lax.fori_loop(0, 8, fine_rows, 0)

    def plain(a, carry):
        for f in range(FIELDS):
            for p in range(DEPTH):
                fn[f, p, pl.ds(pl.multiple_of(a * 8, 8), 8), :] = fo[f, p, pl.ds(a, 8, stride=8), :]
        return carry
    lax.fori_loop(0, 8, plain, 0)
    store = pltpu.make_async_copy(fn, fine_out, out_sem)
    store.start()
    consts[2].wait()
    consts[3].wait()
    load_p.wait()

    def whole(ref, n, sem):
        pltpu.make_async_copy(ref.at[pl.ds(0, n)], ref.at[pl.ds(0, n)], sem).wait()

    def own(tasks):
        whole(got, tasks * SLABS * SLICES, f_recv)
        later = lax.broadcasted_iota(jnp.int32, (SLICES, 128), 0) > 0
        blocks = []
        for t in range(tasks):
            at_row = lambda s: (t * SLABS + s) * SLICES
            jumps = [jnp.where(later, got[at_row(s) : at_row(s) + SLICES], 0.0) for s in range(SLABS)]
            blocks.append(jnp.concatenate(jumps, axis=1))
        modes = product(jnp.concatenate(blocks, axis=0), m2[0], m2[1])
        half = NZ * 2 * KY

        def times(p, re, im):
            gr, gi = pw[p : p + 1, :half], pw[p : p + 1, half:]
            return gr * re - gi * im, gr * im + gi * re

        weight = jnp.where(scan_x2z == 0, 1.0, 2.0) / CELLS
        fixes, sums = [], []
        for t in range(tasks):
            one = modes[t * SLICES : (t + 1) * SLICES]
            re, im = times(0, one[:, :half], one[:, half:])
            for p in range(6):
                zero = jnp.zeros((2**p, half), F32)
                shifted = (jnp.concatenate([zero, v[: -(2**p)]], axis=0) for v in (re, im))
                pr, pi = times(p, *shifted)
                re, im = re + pr, im + pi
            sums.append(jnp.sum(re * re + im * im, axis=1, keepdims=True) * weight)
            fixes.append(jnp.concatenate([re, im], axis=1))
        out = product(jnp.concatenate(fixes, axis=0), m3[0], m3[1])
        lane = lax.broadcasted_iota(jnp.int32, (SLICES, 128), 1)
        for t in range(tasks):
            total = jnp.sum(sums[t], axis=0, keepdims=True)
            for s in range(SLABS):
                piece = out[t * SLICES : (t + 1) * SLICES, s * 128 : (s + 1) * 128]
                row = (t * SLABS + s) * SLICES
                turn[row : row + SLICES] = jnp.where(lane == T_LANE, total, jnp.where(lane == Q_LANE, sums[t], piece))

        def give(tx, carry):
            for ty in range(4):
                for dz in range(2):
                    tz = z - rem(z, 2) + dz
                    for tc in (1, 0):
                        for t in range(tasks):
                            here = turn.at[pl.ds((t * SLABS + tx) * SLICES + (ty * 8 + tz) * 2 + tc, 1)]
                            there = back.at[pl.ds((FIELDS - 1 if t else y) * KX + scan_x2z, 1)]

                            def far():
                                pltpu.make_async_remote_copy(
                                    here, there, c_send, c_recv,
                                    device_id=at(tx, jnp.int32(ty), tz, jnp.int32(tc)), device_id_type=MESH,
                                ).start()

                            if tc == 0:
                                far()
                                continue
                            mine_too = (tx == x) & (y == ty) & (tz == z)
                            pl.when(jnp.logical_not(mine_too))(far)

                            @pl.when(mine_too)
                            def _():
                                pltpu.make_async_copy(here, there, c_recv).start()
            return carry
        lax.fori_loop(0, 4, give, 0)

    pl.when(has_two)(lambda: own(2))
    pl.when(is_owner & jnp.logical_not(has_two))(lambda: own(1))

    whole(back, ROWS, c_recv)
    back_out[...] = back[...]

    pltpu.make_async_copy(halo, halo, hs).wait()

    pass_on.wait_send()

    @pl.when(has_two)
    def _():
        whole(got, 158, f_send)
        whole(turn, 126, c_send)

    @pl.when(is_owner & jnp.logical_not(has_two))
    def _():
        whole(got, 159, f_send)
        whole(turn, 63, c_send)

    @pl.when(jnp.logical_not(is_owner))
    def _():
        whole(got, 160, f_send)

    store.wait()


def main_call(starts, source, t):
    hbm = pl.BlockSpec(memory_space=pltpu.MemorySpace.HBM)
    slab = (FIELDS, DEPTH, NY, NX)
    vm = pltpu.VMEM
    dma = pltpu.SemaphoreType.DMA
    return pl.pallas_call(
        main_kernel,
        out_shape=(jax.ShapeDtypeStruct(slab, F32), jax.ShapeDtypeStruct((ROWS, 128), F32)),
        in_specs=[hbm] * 7,
        out_specs=(pl.BlockSpec(memory_space=pl.ANY), pl.BlockSpec(memory_space=vm)),
        scratch_shapes=[
            vm(slab, F32), vm(slab, F32),
            vm((4, 10, DEPTH, FIELDS, 8, NX), F32),
            vm((4, 2, 8, FIELDS, 8, NX), F32),
            vm(slab, F32), vm(slab, F32),
            vm((32, 128), BF16), vm((2, 512, 128), BF16), vm((2, 512, 512), BF16), vm((2, 512, 512), BF16), vm((8, 512), F32),
            vm((ROWS, 128), F32), vm((ROWS, 128), F32), vm((ROWS, 128), F32),
            vm((2 * SLABS * SLICES, 128), F32), vm((2 * SLABS * SLICES, 128), F32), vm((ROWS, 128), F32),
            dma((3,)), dma((2,)), dma, dma, dma((2, 8)), pltpu.SemaphoreType.REGULAR((8,)),
            dma, dma, dma, dma, dma, dma,
        ],
        compiler_params=pltpu.CompilerParams(collective_id=0, has_side_effects=True, vmem_limit_bytes=24 << 20),
        name="fine_and_scan",
    )(
        *(
            pltpu.with_memory_space_constraint(a, pltpu.MemorySpace.HBM)
            for a in (starts, source, t["cx"], t["m1"], t["m2"], t["m3"], t["powers"])
        )
    )


def last_kernel(fine, back, m4, cinv, ends, slice_norm, total_norm, held, sem):
    rows = back[...]
    e = product(rows, m4[0], m4[1])
    copies = []
    for f in range(FIELDS):
        part = e[f * KX : (f + 1) * KX]
        high, low = split(jnp.concatenate([part[:, :256], part[:, 256:]], axis=0))
        fix = dot(jnp.concatenate([high, low, high], axis=0), cinv[...], ((0,), (0,)))
        held[f] = fine[f] + fix.reshape(DEPTH, NY, NX)
        copies.append(pltpu.make_async_copy(held.at[f], ends.at[0, f], sem))
        copies[-1].start()
    sums = jnp.sum(rows, axis=0, keepdims=True)
    cells = FIELDS * CELLS
    lane = lax.broadcasted_iota(jnp.int32, (1, 128), 1)
    one = jnp.sqrt(jnp.sum(jnp.where(lane == Q_LANE, sums, 0.0), axis=1, keepdims=True) / cells + epsilon)
    every = jnp.sqrt(jnp.sum(jnp.where(lane == T_LANE, sums, 0.0), axis=1, keepdims=True) / (cells * SLICES) + epsilon)
    slice_norm[0] = one[0, 0]
    total_norm[0] = every[0, 0]
    pltpu.make_async_copy(held, ends.at[0], sem).wait()


def last_call(fine, back, t):
    vm = pl.BlockSpec(memory_space=pltpu.VMEM)
    sm = pl.BlockSpec(memory_space=pltpu.SMEM)
    return pl.pallas_call(
        last_kernel,
        out_shape=(
            jax.ShapeDtypeStruct((1, FIELDS, DEPTH, NY, NX), F32),
            jax.ShapeDtypeStruct((1,), F32),
            jax.ShapeDtypeStruct((1,), F32),
        ),
        in_specs=[vm] * 4,
        out_specs=(pl.BlockSpec(memory_space=pltpu.MemorySpace.HBM), sm, sm),
        scratch_shapes=[pltpu.VMEM((FIELDS, DEPTH, NY, NX), F32), pltpu.SemaphoreType.DMA],
        compiler_params=pltpu.CompilerParams(vmem_limit_bytes=8 << 20),
        name="inverse_and_add",
    )(fine, back, t["m4"], t["cinv"])


def solution(mesh):
    held = Mesh(mesh.devices.reshape(4, 8, 2, mesh.shape["space"]), (*TM, X))
    t = tables()

    def shards(starts, source):
        local = {k: jnp.asarray(v) for k, v in t.items()}
        fine, back = main_call(starts, source, local)
        return last_call(fine, back, local)

    return jax.shard_map(
        shards,
        mesh=held,
        in_specs=(P(TM, None, X, None, None), P(None, X, None, None)),
        out_specs=(P(TM, None, X, None, None), P(TM), P()),
        check_vma=False,
    )
```

profile of v0, /device:TPU:1, one launch (start us, length us, event | category | flops | bytes accessed | tf_op | source)
XLA Modules:
  0.0 42.8 jit_solution(4152678807658114429)
XLA Ops:
  0.6 0.0 copy-start
  0.6 0.0 copy-start.1
  0.7 40.4 %fine_and_scan.1 = (f32[5,4,64,128]{3,2,1,0:T(8,128)S(1)}, f32[40,128]{1,0:T(8,128)S(1)}) custom-call(f32[1,5,4,64,128]{4,3,2,1,0:T(8,128)} %starts.1, f32[5,4,64,128]{3,2,1,0:T(8,128)} %source.1, bf16[32,128]{1,0:T(8,128)(2,1)} %constant.14.clone.cx_h, bf16[2,512,128]{2,1,0:T(8,128)(2,1)} %constant.15.clone.m1_h, bf16[2,512,512]{2,1,0:T(8,128)(2,1)} %constant.16.clone.m2_h, ...), custom_call_target="tpu_custom_call" | custom-call | tf_op jit(solution)/shard_map/fine_and_scan/pallas_call | solution.py:456
  41.0 0.0 copy-done
  41.0 0.0 copy-done.1
  41.0 1.7 %inverse_and_add.1 = (f32[1,5,4,64,128]{4,3,2,1,0:T(8,128)}, f32[1]{0:T(128)}, f32[1]{0:T(128)}) custom-call(f32[5,4,64,128]{3,2,1,0:T(8,128)S(1)} %get-tuple-element.5.fine, f32[40,128]{1,0:T(8,128)S(1)} %get-tuple-element.6.back, bf16[2,128,512]{2,1,0:T(8,128)(2,1)S(1)} %copy-done, bf16[48,128]{1,0:T(8,128)(2,1)S(1)} %copy-done.1), custom_call_target="tpu_custom_call" | custom-call | tf_op jit(solution)/shard_map/inverse_and_add/pallas_call | solution.py:506
Async XLA Ops:
  0.6 40.4 %copy-start = (bf16[2,128,512]{2,1,0:T(8,128)(2,1)S(1)}, bf16[2,128,512]{2,1,0:T(8,128)(2,1)}, u32[]{:S(2)}) copy-start(bf16[2,128,512]{2,1,0:T(8,128)(2,1)} %constant.19.clone.m4) | copy-start | bytes 786436
  0.6 40.4 %copy-start.1 = (bf16[48,128]{1,0:T(8,128)(2,1)S(1)}, bf16[48,128]{1,0:T(8,128)(2,1)}, u32[]{:S(2)}) copy-start(bf16[48,128]{1,0:T(8,128)(2,1)} %constant.20.clone.cinv) | copy-start | bytes 36868
where the time goes:
time: 42.9 us; the launch traced here: 42.8 us
  Pallas kernels  42.1 us (98%)
  between operations  0.67 us (2%)
    pallas_call x1, Pallas kernels, main_call(): pl.pallas_call(main_kernel, out_shape=(jax.ShapeDtypeStruct(slab, F32), j...  40.4 us
    pallas_call x1, Pallas kernels, last_call(): pl.pallas_call(last_kernel, out_shape=(jax.ShapeDtypeStruct((1, FIELDS, D...  1.73 us

commit v1 on v0

--- a/solution.py
+++ b/solution.py
@@ -230,7 +230,7 @@
     load_r.wait()
 
     is_owner = c == 1
-    has_two = is_owner & (y == rem(scan_x2z, 4))
+    has_two = is_owner & (y == 0)
     mine = (y * 8 + z) * 2 + c
 
     before = rem(mine + SLICES - 1, SLICES)
@@ -246,7 +246,7 @@
             tx = rem(x + dx, 4)
             kx = tx * 2 + rem(tz, 2)
             for dy in (2, 1, 3, 0, None):
-                ty = rem(kx, 4) if dy is None else rem(y + dy, 4)
+                ty = jnp.int32(0) if dy is None else rem(y + dy, 4)
                 row = (32 if dy is None else ty * KX) + kx
                 here = spec_f.at[pl.ds(row, 1)]
                 there = got.at[pl.ds(slot + (SLABS * SLICES if dy is None else 0), 1)]
@@ -479,8 +479,20 @@
     )
 
 
-def last_kernel(fine, back, m4, cinv, ends, slice_norm, total_norm, held, sem):
+def last_kernel(fine, back, m4, cinv, ends, slice_norm, total_norm, held, norms, sem, norm_sem):
     rows = back[...]
+    sums = jnp.sum(rows, axis=0, keepdims=True)
+    cells = FIELDS * CELLS
+    lane = lax.broadcasted_iota(jnp.int32, (1, 128), 1)
+    one = jnp.sqrt(jnp.sum(jnp.where(lane == Q_LANE, sums, 0.0), axis=1, keepdims=True) / cells + epsilon)
+    every = jnp.sqrt(jnp.sum(jnp.where(lane == T_LANE, sums, 0.0), axis=1, keepdims=True) / (cells * SLICES) + epsilon)
+    norms[0, 0] = one[0, 0]
+    norms[1, 0] = every[0, 0]
+    norm_copies = [
+        pltpu.make_async_copy(norms.at[i], out, norm_sem.at[i]) for i, out in enumerate((slice_norm, total_norm))
+    ]
+    for copy in norm_copies:
+        copy.start()
     e = product(rows, m4[0], m4[1])
     copies = []
     for f in range(FIELDS):
@@ -490,19 +502,14 @@
         held[f] = fine[f] + fix.reshape(DEPTH, NY, NX)
         copies.append(pltpu.make_async_copy(held.at[f], ends.at[0, f], sem))
         copies[-1].start()
-    sums = jnp.sum(rows, axis=0, keepdims=True)
-    cells = FIELDS * CELLS
-    lane = lax.broadcasted_iota(jnp.int32, (1, 128), 1)
-    one = jnp.sqrt(jnp.sum(jnp.where(lane == Q_LANE, sums, 0.0), axis=1, keepdims=True) / cells + epsilon)
-    every = jnp.sqrt(jnp.sum(jnp.where(lane == T_LANE, sums, 0.0), axis=1, keepdims=True) / (cells * SLICES) + epsilon)
-    slice_norm[0] = one[0, 0]
-    total_norm[0] = every[0, 0]
     pltpu.make_async_copy(held, ends.at[0], sem).wait()
+    for copy in norm_copies:
+        copy.wait()
 
 
 def last_call(fine, back, t):
     vm = pl.BlockSpec(memory_space=pltpu.VMEM)
-    sm = pl.BlockSpec(memory_space=pltpu.SMEM)
+    hbm = pl.BlockSpec(memory_space=pltpu.MemorySpace.HBM)
     return pl.pallas_call(
         last_kernel,
         out_shape=(
@@ -511,8 +518,11 @@
             jax.ShapeDtypeStruct((1,), F32),
         ),
         in_specs=[vm] * 4,
-        out_specs=(pl.BlockSpec(memory_space=pltpu.MemorySpace.HBM), sm, sm),
-        scratch_shapes=[pltpu.VMEM((FIELDS, DEPTH, NY, NX), F32), pltpu.SemaphoreType.DMA],
+        out_specs=(hbm, hbm, hbm),
+        scratch_shapes=[
+            pltpu.VMEM((FIELDS, DEPTH, NY, NX), F32), pltpu.SMEM((2, 1), F32),
+            pltpu.SemaphoreType.DMA, pltpu.SemaphoreType.DMA((2,)),
+        ],
         compiler_params=pltpu.CompilerParams(vmem_limit_bytes=8 << 20),
         name="inverse_and_add",
     )(fine, back, t["m4"], t["cinv"])

time: 42.9 us -> 42.4 us (0.988)
  Pallas kernels: 42.1 us -> 41.5 us
    pallas_call x1, Pallas kernels: 1.73 us -> 1.24 us  [last_call(): pl.pallas_call(last_kernel, out_shape=(jax.ShapeDtypeStruct((1, FIELDS, D...]
where the time goes in v1:
time: 42.4 us; the launch traced here: 42.2 us
  Pallas kernels  41.5 us (98%)
  between operations  0.67 us (2%)
    pallas_call x1, Pallas kernels, main_call(): pl.pallas_call(main_kernel, out_shape=(jax.ShapeDtypeStruct(slab, F32), j...  40.3 us
    pallas_call x1, Pallas kernels, last_call(): pl.pallas_call(last_kernel, out_shape=(jax.ShapeDtypeStruct((1, FIELDS, D...  1.24 us

profile of v1, /device:TPU:1, one launch (start us, length us, event | category | flops | bytes accessed | tf_op | source)
XLA Modules:
  0.0 42.2 jit_solution(11383522702010574009)
XLA Ops:
  0.6 0.0 copy-start
  0.6 0.0 copy-start.1
  0.7 40.3 %fine_and_scan.1 = (f32[5,4,64,128]{3,2,1,0:T(8,128)S(1)}, f32[40,128]{1,0:T(8,128)S(1)}) custom-call(f32[1,5,4,64,128]{4,3,2,1,0:T(8,128)} %starts.1, f32[5,4,64,128]{3,2,1,0:T(8,128)} %source.1, bf16[32,128]{1,0:T(8,128)(2,1)} %constant.14.clone.cx_h, bf16[2,512,128]{2,1,0:T(8,128)(2,1)} %constant.15.clone.m1_h, bf16[2,512,512]{2,1,0:T(8,128)(2,1)} %constant.16.clone.m2_h, ...), custom_call_target="tpu_custom_call" | custom-call | tf_op jit(solution)/shard_map/fine_and_scan/pallas_call | solution.py:456
  40.9 0.0 copy-done
  41.0 0.0 copy-done.1
  41.0 1.2 %inverse_and_add.1 = (f32[1,5,4,64,128]{4,3,2,1,0:T(8,128)}, f32[1]{0:T(128)}, f32[1]{0:T(128)}) custom-call(f32[5,4,64,128]{3,2,1,0:T(8,128)S(1)} %get-tuple-element.5.fine, f32[40,128]{1,0:T(8,128)S(1)} %get-tuple-element.6.back, bf16[2,128,512]{2,1,0:T(8,128)(2,1)S(1)} %copy-done, bf16[48,128]{1,0:T(8,128)(2,1)S(1)} %copy-done.1), custom_call_target="tpu_custom_call" | custom-call | tf_op jit(solution)/shard_map/inverse_and_add/pallas_call | solution.py:513
Async XLA Ops:
  0.6 40.3 %copy-start = (bf16[2,128,512]{2,1,0:T(8,128)(2,1)S(1)}, bf16[2,128,512]{2,1,0:T(8,128)(2,1)}, u32[]{:S(2)}) copy-start(bf16[2,128,512]{2,1,0:T(8,128)(2,1)} %constant.19.clone.m4) | copy-start | bytes 786436
  0.6 40.3 %copy-start.1 = (bf16[48,128]{1,0:T(8,128)(2,1)S(1)}, bf16[48,128]{1,0:T(8,128)(2,1)}, u32[]{:S(2)}) copy-start(bf16[48,128]{1,0:T(8,128)(2,1)} %constant.20.clone.cinv) | copy-start | bytes 36868

commit v2 on v1

--- a/solution.py
+++ b/solution.py
@@ -23,8 +23,8 @@
 time_step, diffusion_number = 0.5, 0.08
 advect = {"x": 0.2, "y": 0.15, "z": 0.1}
 epsilon = 1e-06
-GREETINGS = (None, 2, 6, 10, 14, 18, 22, 26)
-PASS_ON = 18
+GREETINGS = (None, 1, 5, 10, 15, 19, 23, 27)
+PASS_ON = 19
 QUARTERS = 4
 ROWS = FIELDS * KX
 Q_LANE, T_LANE = 64, 72
@@ -81,18 +81,20 @@
     imag = -(
         advect["z"] * np.sin(tz)[None, :, None] + advect["y"] * np.sin(ty)[None, None, :] + advect["x"] * np.sin(tx)[:, None, None]
     )
-    g = ((real + 1j * imag) * keep).reshape(KX, NZ * 2 * KY)
+    g = ((real + 1j * imag) * keep)[:, [*range(0, NZ, 2), *range(1, NZ, 2)]].reshape(KX, NZ * 2 * KY)
     powers = np.zeros((KX, 8, 2 * NZ * 2 * KY))
     for p in range(6):
         power = g ** (2**p)
         powers[:, p] = np.concatenate([power.real, power.imag], axis=1)
-    m2 = m2.reshape(SLABS, DEPTH, 2, QUARTERS, 4, 512).transpose(0, 3, 1, 2, 4, 5)
-    m3 = m3.reshape(512, SLABS, DEPTH, 2, QUARTERS, 4).transpose(0, 1, 4, 2, 3, 5)
+    m2 = m2.reshape(SLABS, DEPTH, 2, QUARTERS, 4, 512).transpose(0, 3, 1, 2, 4, 5).reshape(SLABS, 128, 2, NZ, 2 * KY)
+    m3 = m3.reshape(512, SLABS, DEPTH, 2, QUARTERS, 4).transpose(0, 1, 4, 2, 3, 5).reshape(2, NZ, 2 * KY, SLABS, 128)
+    m2 = np.stack([m2[:2, :, :, odd::2].reshape(256, 256) for odd in range(2)])
+    m3 = np.stack([m3[:, odd::2, :, :2].reshape(256, 256) for odd in range(2)])
     return dict(
         cx=np.concatenate(halves(cx)),
         m1=np.stack(halves(m1.reshape(512, 128))),
-        m2=np.stack(halves(m2.reshape(512, 512))),
-        m3=np.stack(halves(m3.reshape(512, 512))),
+        m2=np.stack(halves(m2)),
+        m3=np.stack(halves(m3)),
         powers=powers.astype(np.float32),
         m4=np.stack(halves(m4.reshape(128, 512))),
         cinv=np.concatenate([halves(cinv)[0], halves(cinv)[0], halves(cinv)[1]]),
@@ -361,12 +363,13 @@
     def own(tasks):
         whole(got, tasks * SLABS * SLICES, f_recv)
         later = lax.broadcasted_iota(jnp.int32, (SLICES, 128), 0) > 0
-        blocks = []
+        blocks = ([], [])
         for t in range(tasks):
             at_row = lambda s: (t * SLABS + s) * SLICES
             jumps = [jnp.where(later, got[at_row(s) : at_row(s) + SLICES], 0.0) for s in range(SLABS)]
-            blocks.append(jnp.concatenate(jumps, axis=1))
-        modes = product(jnp.concatenate(blocks, axis=0), m2[0], m2[1])
+            blocks[0].append(jnp.concatenate([jumps[0] + jumps[2], jumps[1] + jumps[3]], axis=1))
+            blocks[1].append(jnp.concatenate([jumps[0] - jumps[2], jumps[1] - jumps[3]], axis=1))
+        even, odd = (product(jnp.concatenate(blocks[i], axis=0), m2[0, i], m2[1, i]) for i in range(2))
         half = NZ * 2 * KY
 
         def times(p, re, im):
@@ -376,21 +379,22 @@
         weight = jnp.where(scan_x2z == 0, 1.0, 2.0) / CELLS
         fixes, sums = [], []
         for t in range(tasks):
-            one = modes[t * SLICES : (t + 1) * SLICES]
-            re, im = times(0, one[:, :half], one[:, half:])
+            parts = [v[t * SLICES : (t + 1) * SLICES] for v in (even, odd)]
+            re, im = times(0, *(jnp.concatenate([v[:, i : i + 128] for v in parts], axis=1) for i in (0, 128)))
             for p in range(6):
                 zero = jnp.zeros((2**p, half), F32)
                 shifted = (jnp.concatenate([zero, v[: -(2**p)]], axis=0) for v in (re, im))
                 pr, pi = times(p, *shifted)
                 re, im = re + pr, im + pi
             sums.append(jnp.sum(re * re + im * im, axis=1, keepdims=True) * weight)
-            fixes.append(jnp.concatenate([re, im], axis=1))
-        out = product(jnp.concatenate(fixes, axis=0), m3[0], m3[1])
+            fixes.append([jnp.concatenate([re[:, i : i + 128], im[:, i : i + 128]], axis=1) for i in (0, 128)])
+        even, odd = (product(jnp.concatenate([v[i] for v in fixes], axis=0), m3[0, i], m3[1, i]) for i in range(2))
+        out = (even + odd, even - odd)
         lane = lax.broadcasted_iota(jnp.int32, (SLICES, 128), 1)
         for t in range(tasks):
             total = jnp.sum(sums[t], axis=0, keepdims=True)
             for s in range(SLABS):
-                piece = out[t * SLICES : (t + 1) * SLICES, s * 128 : (s + 1) * 128]
+                piece = out[s // 2][t * SLICES : (t + 1) * SLICES, s % 2 * 128 : s % 2 * 128 + 128]
                 row = (t * SLABS + s) * SLICES
                 turn[row : row + SLICES] = jnp.where(lane == T_LANE, total, jnp.where(lane == Q_LANE, sums[t], piece))
 
@@ -463,7 +467,7 @@
             vm((4, 10, DEPTH, FIELDS, 8, NX), F32),
             vm((4, 2, 8, FIELDS, 8, NX), F32),
             vm(slab, F32), vm(slab, F32),
-            vm((32, 128), BF16), vm((2, 512, 128), BF16), vm((2, 512, 512), BF16), vm((2, 512, 512), BF16), vm((8, 512), F32),
+            vm((32, 128), BF16), vm((2, 512, 128), BF16), vm((2, 2, 256, 256), BF16), vm((2, 2, 256, 256), BF16), vm((8, 512), F32),
             vm((ROWS, 128), F32), vm((ROWS, 128), F32), vm((ROWS, 128), F32),
             vm((2 * SLABS * SLICES, 128), F32), vm((2 * SLABS * SLICES, 128), F32), vm((ROWS, 128), F32),
             dma((3,)), dma((2,)), dma, dma, dma((2, 8)), pltpu.SemaphoreType.REGULAR((8,)),
@@ -481,6 +485,15 @@
 
 def last_kernel(fine, back, m4, cinv, ends, slice_norm, total_norm, held, norms, sem, norm_sem):
     rows = back[...]
+    e = product(rows, m4[0], m4[1])
+    copies = []
+    for f in range(FIELDS):
+        part = e[f * KX : (f + 1) * KX]
+        high, low = split(jnp.concatenate([part[:, :256], part[:, 256:]], axis=0))
+        fix = dot(jnp.concatenate([high, low, high], axis=0), cinv[...], ((0,), (0,)))
+        held[f] = fine[f] + fix.reshape(DEPTH, NY, NX)
+        copies.append(pltpu.make_async_copy(held.at[f], ends.at[0, f], sem))
+        copies[-1].start()
     sums = jnp.sum(rows, axis=0, keepdims=True)
     cells = FIELDS * CELLS
     lane = lax.broadcasted_iota(jnp.int32, (1, 128), 1)
@@ -493,15 +506,6 @@
     ]
     for copy in norm_copies:
         copy.start()
-    e = product(rows, m4[0], m4[1])
-    copies = []
-    for f in range(FIELDS):
-        part = e[f * KX : (f + 1) * KX]
-        high, low = split(jnp.concatenate([part[:, :256], part[:, 256:]], axis=0))
-        fix = dot(jnp.concatenate([high, low, high], axis=0), cinv[...], ((0,), (0,)))
-        held[f] = fine[f] + fix.reshape(DEPTH, NY, NX)
-        copies.append(pltpu.make_async_copy(held.at[f], ends.at[0, f], sem))
-        copies[-1].start()
     pltpu.make_async_copy(held, ends.at[0], sem).wait()
     for copy in norm_copies:
         copy.wait()

time: 42.4 us -> 42.1 us (level)
  no operation moved by 1% of the time
where the time goes in v2:
time: 42.1 us; the launch traced here: 42 us
  Pallas kernels  41.3 us (98%)
  between operations  0.67 us (2%)
    pallas_call x1, Pallas kernels, main_call(): pl.pallas_call(main_kernel, out_shape=(jax.ShapeDtypeStruct(slab, F32), j...  40.1 us
    pallas_call x1, Pallas kernels, last_call(): pl.pallas_call(last_kernel, out_shape=(jax.ShapeDtypeStruct((1, FIELDS, D...  1.24 us

profile of v2, /device:TPU:1, one launch (start us, length us, event | category | flops | bytes accessed | tf_op | source)
XLA Modules:
  0.0 42.0 jit_solution(10412304705777000382)
XLA Ops:
  0.6 0.0 copy-start
  0.6 0.0 copy-start.1
  0.7 40.1 %fine_and_scan.1 = (f32[5,4,64,128]{3,2,1,0:T(8,128)S(1)}, f32[40,128]{1,0:T(8,128)S(1)}) custom-call(f32[1,5,4,64,128]{4,3,2,1,0:T(8,128)} %starts.1, f32[5,4,64,128]{3,2,1,0:T(8,128)} %source.1, bf16[32,128]{1,0:T(8,128)(2,1)} %constant.14.clone.cx_h, bf16[2,512,128]{2,1,0:T(8,128)(2,1)} %constant.15.clone.m1_h, ...), custom_call_target="tpu_custom_call" | custom-call | tf_op jit(solution)/shard_map/fine_and_scan/pallas_call | solution.py:460
  40.7 0.0 copy-done
  40.7 0.0 copy-done.1
  40.8 1.2 %inverse_and_add.1 = (f32[1,5,4,64,128]{4,3,2,1,0:T(8,128)}, f32[1]{0:T(128)}, f32[1]{0:T(128)}) custom-call(f32[5,4,64,128]{3,2,1,0:T(8,128)S(1)} %get-tuple-element.5.fine, f32[40,128]{1,0:T(8,128)S(1)} %get-tuple-element.6.back, bf16[2,128,512]{2,1,0:T(8,128)(2,1)S(1)} %copy-done, bf16[48,128]{1,0:T(8,128)(2,1)S(1)} %copy-done.1), custom_call_target="tpu_custom_call" | custom-call | tf_op jit(solution)/shard_map/inverse_and_add/pallas_call | solution.py:517
Async XLA Ops:
  0.6 40.1 %copy-start = (bf16[2,128,512]{2,1,0:T(8,128)(2,1)S(1)}, bf16[2,128,512]{2,1,0:T(8,128)(2,1)}, u32[]{:S(2)}) copy-start(bf16[2,128,512]{2,1,0:T(8,128)(2,1)} %constant.19.clone.m4) | copy-start | bytes 786436
  0.6 40.1 %copy-start.1 = (bf16[48,128]{1,0:T(8,128)(2,1)S(1)}, bf16[48,128]{1,0:T(8,128)(2,1)}, u32[]{:S(2)}) copy-start(bf16[48,128]{1,0:T(8,128)(2,1)} %constant.20.clone.cinv) | copy-start | bytes 36868

commit v3 on v2

--- a/solution.py
+++ b/solution.py
@@ -117,14 +117,13 @@
     return both[:m] + both[m:] + dot(xh, low)
 
 
-def low_modes(field_rows, cx, m1):
-    out = []
-    for f in range(FIELDS):
-        high, low = split(field_rows(f))
-        a = dot(cx, high, ((1,), (1,)))
-        a = a[:16] + a[16:] + dot(cx[:16], low, ((1,), (1,)))
-        out.append(jnp.concatenate([a[:KX], a[KX:]], axis=1))
-    return product(jnp.concatenate(out, axis=0), m1[0], m1[1])
+def low_modes(rows, cx, m1):
+    high, low = split(rows)
+    a = dot(cx, high, ((1,), (1,)))
+    a = a[:16] + a[16:] + dot(cx[:16], low, ((1,), (1,)))
+    n = DEPTH * NY
+    fields = [jnp.concatenate([a[:KX, f * n : (f + 1) * n], a[KX:, f * n : (f + 1) * n]], axis=1) for f in range(FIELDS)]
+    return product(jnp.concatenate(fields, axis=0), m1[0], m1[1])
 
 
 def rem(a, n):
@@ -227,7 +226,7 @@
     consts[0].wait()
     consts[1].wait()
     spec_s[...] = low_modes(
-        lambda f: jnp.concatenate([q[0, 1:9, p, f].reshape(NY, NX) for p in range(DEPTH)], axis=0), cx[...], m1
+        jnp.concatenate([q[0, 1:9, p, f].reshape(NY, NX) for f in range(FIELDS) for p in range(DEPTH)], axis=0), cx[...], m1
     )
     load_r.wait()
 
@@ -336,7 +335,7 @@
         stage(j)
     pl.semaphore_wait(rounds.at[7], 2)
 
-    modes = low_modes(lambda f: fo[f].reshape(DEPTH * NY, NX), cx[...], m1)
+    modes = low_modes(fo[...].reshape(FIELDS * DEPTH * NY, NX), cx[...], m1)
     pass_on.wait_recv()
     spec_f[...] = modes - after[...]
 

time: 42.1 us -> 42.2 us (level)
  no operation moved by 1% of the time
where the time goes in v3:
time: 42.2 us; the launch traced here: 42 us
  Pallas kernels  41.3 us (98%)
  between operations  0.67 us (2%)
    pallas_call x1, Pallas kernels, main_call(): pl.pallas_call(main_kernel, out_shape=(jax.ShapeDtypeStruct(slab, F32), j...  40.1 us
    pallas_call x1, Pallas kernels, last_call(): pl.pallas_call(last_kernel, out_shape=(jax.ShapeDtypeStruct((1, FIELDS, D...  1.24 us

profile of v3, /device:TPU:1, one launch (start us, length us, event | category | flops | bytes accessed | tf_op | source)
XLA Modules:
  0.0 42.0 jit_solution(6461793516761768834)
XLA Ops:
  0.6 0.0 copy-start
  0.6 0.0 copy-start.1
  0.7 40.1 %fine_and_scan.1 = (f32[5,4,64,128]{3,2,1,0:T(8,128)S(1)}, f32[40,128]{1,0:T(8,128)S(1)}) custom-call(f32[1,5,4,64,128]{4,3,2,1,0:T(8,128)} %starts.1, f32[5,4,64,128]{3,2,1,0:T(8,128)} %source.1, bf16[32,128]{1,0:T(8,128)(2,1)} %constant.14.clone.cx_h, bf16[2,512,128]{2,1,0:T(8,128)(2,1)} %constant.15.clone.m1_h, ...), custom_call_target="tpu_custom_call" | custom-call | tf_op jit(solution)/shard_map/fine_and_scan/pallas_call | solution.py:459
  40.7 0.0 copy-done
  40.8 0.0 copy-done.1
  40.8 1.2 %inverse_and_add.1 = (f32[1,5,4,64,128]{4,3,2,1,0:T(8,128)}, f32[1]{0:T(128)}, f32[1]{0:T(128)}) custom-call(f32[5,4,64,128]{3,2,1,0:T(8,128)S(1)} %get-tuple-element.5.fine, f32[40,128]{1,0:T(8,128)S(1)} %get-tuple-element.6.back, bf16[2,128,512]{2,1,0:T(8,128)(2,1)S(1)} %copy-done, bf16[48,128]{1,0:T(8,128)(2,1)S(1)} %copy-done.1), custom_call_target="tpu_custom_call" | custom-call | tf_op jit(solution)/shard_map/inverse_and_add/pallas_call | solution.py:516
Async XLA Ops:
  0.6 40.1 %copy-start = (bf16[2,128,512]{2,1,0:T(8,128)(2,1)S(1)}, bf16[2,128,512]{2,1,0:T(8,128)(2,1)}, u32[]{:S(2)}) copy-start(bf16[2,128,512]{2,1,0:T(8,128)(2,1)} %constant.19.clone.m4) | copy-start | bytes 786436
  0.6 40.1 %copy-start.1 = (bf16[48,128]{1,0:T(8,128)(2,1)S(1)}, bf16[48,128]{1,0:T(8,128)(2,1)}, u32[]{:S(2)}) copy-start(bf16[48,128]{1,0:T(8,128)(2,1)} %constant.20.clone.cinv) | copy-start | bytes 36868

commit v4 on v2

--- a/solution.py
+++ b/solution.py
@@ -341,9 +341,11 @@
     spec_f[...] = modes - after[...]
 
     def fine_rows(i, carry):
-        spread(picked(i, (0, 1, 7, 2, 6, 3, 5, 4)))
+        spread(picked(i, (7, 2, 6, 3, 5, 4)))
         return carry
-    lax.fori_loop(0, 8, fine_rows, 0)
+    spread(jnp.int32(0))
+    spread(jnp.int32(1))
+    lax.fori_loop(0, 6, fine_rows, 0)
 
     def plain(a, carry):
         for f in range(FIELDS):

time: 42.1 us -> 42.1 us (level)
  no operation moved by 1% of the time
where the time goes in v4:
time: 42.1 us; the launch traced here: 42 us
  Pallas kernels  41.3 us (98%)
  between operations  0.67 us (2%)
    pallas_call x1, Pallas kernels, main_call(): pl.pallas_call(main_kernel, out_shape=(jax.ShapeDtypeStruct(slab, F32), j...  40 us
    pallas_call x1, Pallas kernels, last_call(): pl.pallas_call(last_kernel, out_shape=(jax.ShapeDtypeStruct((1, FIELDS, D...  1.24 us

profile of v4, /device:TPU:1, one launch (start us, length us, event | category | flops | bytes accessed | tf_op | source)
XLA Modules:
  0.0 42.0 jit_solution(8329765104484267361)
XLA Ops:
  0.6 0.0 copy-start
  0.6 0.0 copy-start.1
  0.7 40.0 %fine_and_scan.1 = (f32[5,4,64,128]{3,2,1,0:T(8,128)S(1)}, f32[40,128]{1,0:T(8,128)S(1)}) custom-call(f32[1,5,4,64,128]{4,3,2,1,0:T(8,128)} %starts.1, f32[5,4,64,128]{3,2,1,0:T(8,128)} %source.1, bf16[32,128]{1,0:T(8,128)(2,1)} %constant.14.clone.cx_h, bf16[2,512,128]{2,1,0:T(8,128)(2,1)} %constant.15.clone.m1_h, ...), custom_call_target="tpu_custom_call" | custom-call | tf_op jit(solution)/shard_map/fine_and_scan/pallas_call | solution.py:462
  40.7 0.0 copy-done
  40.7 0.0 copy-done.1
  40.7 1.2 %inverse_and_add.1 = (f32[1,5,4,64,128]{4,3,2,1,0:T(8,128)}, f32[1]{0:T(128)}, f32[1]{0:T(128)}) custom-call(f32[5,4,64,128]{3,2,1,0:T(8,128)S(1)} %get-tuple-element.5.fine, f32[40,128]{1,0:T(8,128)S(1)} %get-tuple-element.6.back, bf16[2,128,512]{2,1,0:T(8,128)(2,1)S(1)} %copy-done, bf16[48,128]{1,0:T(8,128)(2,1)S(1)} %copy-done.1), custom_call_target="tpu_custom_call" | custom-call | tf_op jit(solution)/shard_map/inverse_and_add/pallas_call | solution.py:519
Async XLA Ops:
  0.6 40.1 %copy-start = (bf16[2,128,512]{2,1,0:T(8,128)(2,1)S(1)}, bf16[2,128,512]{2,1,0:T(8,128)(2,1)}, u32[]{:S(2)}) copy-start(bf16[2,128,512]{2,1,0:T(8,128)(2,1)} %constant.19.clone.m4) | copy-start | bytes 786436
  0.6 40.1 %copy-start.1 = (bf16[48,128]{1,0:T(8,128)(2,1)S(1)}, bf16[48,128]{1,0:T(8,128)(2,1)}, u32[]{:S(2)}) copy-start(bf16[48,128]{1,0:T(8,128)(2,1)} %constant.20.clone.cinv) | copy-start | bytes 36868
